TPU v7x, 32 devices: a whole 2x2x4 slice. The times are simulated.
32 devices in a mesh: mem: 16 (over z, y, core), band: 2 (over x).
Axes of the slice: x: 2, y: 2, z: 4, core: 2. Of those that a mesh axis runs over, the one named last changes fastest.
Arguments:
- ensemble: bfloat16 [16, 12, 32, 128], P('mem', None, 'band'), may hold values from -6 to 6
- alpha: float32 [16, 12, 32, 128], P('mem', None, 'band'), may hold values from -6 to 6
- lat_lower: int32 [96], P('band'), may hold values from -1 to 15, as said below
- lat_weight: float32 [96], P('band'), may hold values from 0 to 1
- background: float32 [12, 32, 1152], P(None, ('band', 'mem')), may hold values from -6 to 6
- obs_cell: int32 [32, 256], P(('band', 'mem')), may hold values from 0 to 1151
- obs_value: float32 [12, 32, 256], P(None, ('band', 'mem')), may hold values from -6 to 6
- obs_precision: float32 [32, 256], P(('band', 'mem')), may hold values from 1 to 10
Outputs:
- advected: float32 [12, 32, 1152], P(None, ('band', 'mem'))
- gradient: float32 [16, 12, 32, 128], P('mem', None, 'band')
Inputs may be any that keep to these rules, and one draw needn't show every extreme that they name: `lat_lower`: fine rows of the first band use lower rows from 0, those of the last band up to 14 of their band, so that their upper row reaches 15; other bands reach -1 and 15. `obs_cell`: the cell is r * 24 + c for fine row r and column c within the tile.
All inputs are finite; a program needn't handle non-finite values.
Results may differ from a plain program's by a relative error of at most 0.0004.
Values sent between devices are 32-bit elements; how exact they have to be, the bound alone decides.
A program may use at most 64 MiB of HBM per device.

v0:
```python
import math

import jax
import jax.numpy as jnp
from jax import lax
from jax.sharding import PartitionSpec as P

advect_rate = 0.25
highest = lax.Precision.HIGHEST


def padded_2(array, sides, width, wrap):
    for axis, dim in sides:
        size, length = (lax.axis_size(axis), array.shape[dim])
        up = [(i, (i + 1) % size) for i in range(size if wrap else size - 1)]
        down = [(j, i) for i, j in up]
        last = lax.slice_in_dim(array, length - width, length, axis=dim)
        initial = lax.slice_in_dim(array, 0, width, axis=dim)
        before = lax.ppermute(last, axis, up)
        after = lax.ppermute(initial, axis, down)
        array = jnp.concatenate([before, array, after], axis=dim)
    return array


def band_rows(grid_field):
    return padded_2(grid_field, (("band", 2),), 1, False)


def smooth_local(grid_field):
    padded = band_rows(grid_field)
    grid_field = 0.25 * padded[:, :, :-2] + 0.5 * padded[:, :, 1:-1] + 0.25 * padded[:, :, 2:]
    return 0.25 * jnp.roll(grid_field, 1, 3) + 0.5 * grid_field + 0.25 * jnp.roll(grid_field, -1, 3)


def coarse_frame(grid_field):
    return padded_2(grid_field, (("band", 1), ("mem", 2)), 1, True)


def state_slope(grid_field):
    padded = padded_2(grid_field, (("mem", 2),), 1, True)
    return 0.5 * (padded[:, :, 2:] - padded[:, :, :-2])


def flux_slope(grid_field):
    padded = padded_2(grid_field, (("mem", 2),), 1, True)
    return 0.5 * (padded[:, :, 2:] - padded[:, :, :-2])


def latitude_local(lat_lower, lat_weight, coarse_rows):
    padded = jnp.arange(coarse_rows + 2, dtype=jnp.int32)[None, :]
    lower_row = lat_lower[:, None] + 1
    weight = lat_weight[:, None]
    return (1.0 - weight) * (padded == lower_row) + weight * (padded == lower_row + 1)


def longitude_local(coarse_cols, fine_cols, count):
    fine_ratio = fine_cols // coarse_cols
    fine_index = jnp.arange(count, dtype=jnp.int32)
    numerator = 2 * fine_index + 1 + fine_ratio
    upper_col = numerator // (2 * fine_ratio)
    fraction = (numerator % (2 * fine_ratio)).astype(jnp.float32) / (2 * fine_ratio)
    padded = jnp.arange(coarse_cols + 2, dtype=jnp.int32)[:, None]
    return (1.0 - fraction)[None, :] * (padded == upper_col[None, :]) + fraction[None, :] * (
        padded == upper_col[None, :] + 1
    )


def shards(ensemble, alpha, lat_lower, lat_weight, background, obs_cell, obs_value, obs_precision):
    groups = lax.axis_size("mem")
    member_scale = 1.0 / math.sqrt(ensemble.shape[0] * groups - 1)
    levels = ensemble.shape[1]
    coarse_rows = ensemble.shape[2]
    coarse_lon = ensemble.shape[3]
    block_cols = coarse_lon // groups
    fine_rows = lat_lower.shape[0]
    cell_count = background.shape[2]
    fine_cols = cell_count // fine_rows
    back_grid = background.reshape(levels, fine_rows, fine_cols)
    members_f = ensemble.astype(jnp.float32)
    partial_value = jnp.sum(smooth_local(alpha) * members_f, axis=0) * member_scale
    increment = lax.psum_scatter(partial_value, "mem", scatter_dimension=2, tiled=True)
    lat_table = latitude_local(lat_lower, lat_weight, coarse_rows)
    lon_table = longitude_local(block_cols, fine_cols, fine_cols)
    bordered = coarse_frame(increment)
    lat_rows = jnp.einsum("ik,lkc->lic", lat_table, bordered, precision=highest)
    fine_incr = jnp.einsum("lic,cj->lij", lat_rows, lon_table, precision=highest)
    fine_state = back_grid + fine_incr
    lon_slope = state_slope(fine_state)
    advected = fine_state - advect_rate * fine_state * lon_slope
    flat_model = advected.reshape(levels, cell_count)
    obs_onehot = (obs_cell[0][:, None] == jnp.arange(cell_count, dtype=jnp.int32)[None, :]).astype(
        jnp.float32
    )
    observed = jnp.einsum("lc,nc->ln", flat_model, obs_onehot, precision=highest)
    weighted = obs_precision[0][None, :] * (observed - obs_value[:, 0, :])
    cotangent = jnp.dot(weighted, obs_onehot, precision=highest).reshape(
        levels, fine_rows, fine_cols
    )
    adj_flux = flux_slope(fine_state * cotangent)
    adjoint = cotangent - advect_rate * (cotangent * lon_slope - adj_flux)
    back_rows = jnp.einsum("lij,cj->lic", adjoint, lon_table, precision=highest)
    spread_back = jnp.einsum("ik,lic->lkc", lat_table, back_rows, precision=highest)
    last_row = coarse_rows - 1
    last_col = block_cols - 1
    framed = coarse_frame(spread_back)
    inner_rows = slice(2, coarse_rows + 2)
    inner_cols = slice(2, block_cols + 2)
    far_row = coarse_rows + 3
    far_col = block_cols + 3
    own_block = framed[:, inner_rows, inner_cols]
    own_block = (
        own_block.at[:, 0, :]
        .add(framed[:, 0, inner_cols])
        .at[:, last_row, :]
        .add(framed[:, far_row, inner_cols])
    )
    own_block = (
        own_block.at[:, :, 0]
        .add(framed[:, inner_rows, 0])
        .at[:, :, last_col]
        .add(framed[:, inner_rows, far_col])
    )
    own_block = (
        own_block.at[:, 0, 0].add(framed[:, 0, 0]).at[:, 0, last_col].add(framed[:, 0, far_col])
    )
    own_block = (
        own_block.at[:, last_row, 0]
        .add(framed[:, far_row, 0])
        .at[:, last_row, last_col]
        .add(framed[:, far_row, far_col])
    )
    coarse_gradient = lax.all_gather(own_block, "mem", axis=2, tiled=True)
    gradient = smooth_local(members_f * coarse_gradient[None] * member_scale)
    return (advected.reshape(levels, 1, cell_count), gradient)


def solution(mesh):
    return jax.shard_map(
        shards,
        mesh=mesh,
        in_specs=(
            P("mem", None, "band", None),
            P("mem", None, "band", None),
            P("band"),
            P("band"),
            P(None, ("band", "mem"), None),
            P(("band", "mem"), None),
            P(None, ("band", "mem"), None),
            P(("band", "mem"), None),
        ),
        out_specs=(P(None, ("band", "mem"), None), P("mem", None, "band", None)),
        check_vma=False,
    )
```

profile of v0, /device:TPU:0, one launch (start us, length us, event | category | flops | bytes accessed | tf_op | source)
XLA Modules:
  0.0 163.6 jit_solution(8176199175990151694)
XLA Ops:
  8.1 4.9 %collective-permute-start = (f32[1,12,1,128]{3,2,1,0:T(1,128)S(1)}, f32[1,12,1,128]{3,2,1,0:T(1,128)S(1)}, u32[]{:S(2)}, u32[]{:S(2)}) collective-permute-start(f32[1,12,1,128]{3,2,1,0:T(1,128)S(1)} %get-tuple-element.128), channel_id=1, source_target_pairs={{0,1},{2,3},{4,5},{6,7},{8,9},{10,11},{12,13},{14,15},{16,17},{18,... | collective-permute-start | bytes 18440 | tf_op jit(solution)/shard_map/ppermute | solution.py:19
  12.9 1.3 collective-permute-start.1
  14.9 3.6 %collective-permute-done.1 = f32[1,12,1,128]{3,2,1,0:T(1,128)S(1)} collective-permute-done((f32[1,12,1,128]{3,2,1,0:T(1,128)S(1)}, f32[1,12,1,128]{3,2,1,0:T(1,128)S(1)}, u32[]{:S(2)}, u32[]{:S(2)}) %collective-permute-start.1) | collective-permute-done | bytes 6176 | tf_op jit(solution)/shard_map/ppermute | solution.py:20
  18.5 1.1 fusion.25
  19.9 1.4 copy.124
  21.4 58.1 %reduce-scatter.2.cloned.1.call-done = f32[12,16,8]{1,0,2:T(8,128)} async-done(((f32[12,16,128]{1,0,2:T(8,128)}), f32[12,16,8]{1,0,2:T(8,128)}) %reduce-scatter.2.cloned.1.call-update) | async-done | bytes 6160 | tf_op jit(solution)/shard_map/reduce_scatter | solution.py:81
  79.5 1.0 fusion.92
  80.5 1.4 collective-permute-start.2
  83.4 1.4 collective-permute-done.2
  84.8 1.3 collective-permute-done.3
  86.4 4.4 %collective-permute-start.5 = (f32[12,18,1]{1,2,0:T(1,128)S(1)}, f32[12,18,1]{1,2,0:T(1,128)S(1)}, u32[]{:S(2)}, u32[]{:S(2)}) collective-permute-start(f32[12,18,1]{1,2,0:T(1,128)S(1)} %get-tuple-element.117), channel_id=1, source_target_pairs={{2,0},{4,2},{6,4},{8,6},{10,8},{12,10},{14,12},{16,14},{18,16},{20... | collective-permute-start | bytes 2600 | tf_op jit(solution)/shard_map/ppermute | solution.py:20
  92.8 4.5 %collective-permute-start.6 = (f32[12,48,1]{1,2,0:T(1,128)S(1)}, f32[12,48,1]{1,2,0:T(1,128)S(1)}, u32[]{:S(2)}, u32[]{:S(2)}) collective-permute-start(f32[12,48,1]{1,2,0:T(1,128)S(1)} %get-tuple-element.114), channel_id=1, source_target_pairs={{2,0},{4,2},{6,4},{8,6},{10,8},{12,10},{14,12},{16,14},{18,16},{20... | collective-permute-start | bytes 6920 | tf_op jit(solution)/shard_map/ppermute | solution.py:20
  97.3 1.3 collective-permute-done.6
  98.6 4.4 %collective-permute-done.7 = f32[12,48,1]{1,2,0:T(1,128)S(1)} collective-permute-done((f32[12,48,1]{1,2,0:T(1,128)S(1)}, f32[12,48,1]{1,2,0:T(1,128)S(1)}, u32[]{:S(2)}, u32[]{:S(2)}) %collective-permute-start.7) | collective-permute-done | bytes 2336 | tf_op jit(solution)/shard_map/ppermute | solution.py:19
  106.5 4.5 %collective-permute-done.9 = f32[12,48,1]{1,2,0:T(1,128)S(1)} collective-permute-done((f32[12,48,1]{1,2,0:T(1,128)S(1)}, f32[12,48,1]{1,2,0:T(1,128)S(1)}, u32[]{:S(2)}, u32[]{:S(2)}) %collective-permute-start.9) | collective-permute-done | bytes 2336 | tf_op jit(solution)/shard_map/ppermute | solution.py:19
  112.4 1.3 collective-permute-start.11
  114.4 1.8 %collective-permute-done.10 = f32[12,1,10]{1,0,2:T(8,128)S(1)} collective-permute-done((f32[12,1,10]{1,0,2:T(8,128)S(1)}, f32[12,1,10]{1,0,2:T(8,128)S(1)}, u32[]{:S(2)}, u32[]{:S(2)}) %collective-permute-start.10) | collective-permute-done | bytes 512 | tf_op jit(solution)/shard_map/ppermute | solution.py:19
  117.1 4.4 %collective-permute-start.13 = (f32[12,20,1]{1,0,2:T(8,128)S(1)}, f32[12,20,1]{1,0,2:T(8,128)S(1)}, u32[]{:S(2)}, u32[]{:S(2)}) collective-permute-start(f32[12,20,1]{1,0,2:T(8,128)S(1)} %get-tuple-element.110), channel_id=1, source_target_pairs={{2,0},{4,2},{6,4},{8,6},{10,8},{12,10},{14,12},{16,14},{18,16},{20... | collective-permute-start | bytes 2888 | tf_op jit(solution)/shard_map/ppermute | solution.py:20
  123.1 2.0 %add_select_fusion = f32[12,1,1]{1,0,2:T(8,128)S(1)} fusion(f32[12,20,1]{1,0,2:T(8,128)S(1)} %collective-permute-done.13, f32[12,16,8]{1,0,2:T(8,128)S(1)} %scatter-add.34, s32[]{:T(128)} %bitcast.7, s32[]{:T(128)} %bitcast.8, pred[]{:T(512)} %and_reduce_fusion), kind=kLoop, calls=%fused_computation.67 | loop fusion | flops 24 | bytes 153 | tf_op jit(solution)/shard_map/select.13
  125.1 1.4 scatter-add.35
  126.8 20.1 %all_gather.3 = f32[12,16,128]{1,2,0:T(8,128)S(1)} all-gather(f32[12,16,8]{1,2,0:T(8,128)S(1)} %copy.135), channel_id=1, replica_groups=mesh['mem'=16,'band'=2] {'mem'}, dimensions={2}, use_global_device_ids=true | all-gather | bytes 104448 | tf_op jit(solution)/shard_map/all_gather | solution.py:132
  147.2 3.1 %collective-permute-start.14 = (f32[1,12,1,128]{3,2,1,0:T(1,128)S(1)}, f32[1,12,1,128]{3,2,1,0:T(1,128)S(1)}, u32[]{:S(2)}, u32[]{:S(2)}) collective-permute-start(f32[1,12,1,128]{3,2,1,0:T(1,128)S(1)} %get-tuple-element.122), channel_id=1, source_target_pairs={{0,1},{2,3},{4,5},{6,7},{8,9},{10,11},{12,13},{14,15},{16,17},{18,... | collective-permute-start | bytes 18440 | tf_op jit(solution)/shard_map/ppermute | solution.py:19
  150.3 1.3 collective-permute-start.15
  152.4 3.4 %collective-permute-done.15 = f32[1,12,1,128]{3,2,1,0:T(1,128)S(1)} collective-permute-done((f32[1,12,1,128]{3,2,1,0:T(1,128)S(1)}, f32[1,12,1,128]{3,2,1,0:T(1,128)S(1)}, u32[]{:S(2)}, u32[]{:S(2)}) %collective-permute-start.15) | collective-permute-done | bytes 6176 | tf_op jit(solution)/shard_map/ppermute | solution.py:20
  (90 shorter events, 16.0 us)
Async XLA Ops:
  7.2 12.6 %copy-start = (f32[1,12,16,128]{3,2,1,0:T(8,128)S(1)}, f32[1,12,16,128]{3,2,1,0:T(8,128)}, u32[]{:S(2)}) copy-start(f32[1,12,16,128]{3,2,1,0:T(8,128)} %param.25) | copy-start | bytes 294916
  7.2 12.6 %copy-start.1 = (bf16[1,12,16,128]{3,2,1,0:T(8,128)(2,1)S(1)}, bf16[1,12,16,128]{3,2,1,0:T(8,128)(2,1)}, u32[]{:S(2)}) copy-start(bf16[1,12,16,128]{3,2,1,0:T(8,128)(2,1)} %param.24) | copy-start | bytes 147460
  7.2 72.3 %reduce-scatter.2.cloned.1.call-start = ((), (), s32[]{:S(2)}) async-start(), calls=%async_computation.1 | async-start | bytes 1114112 | tf_op jit(solution)/shard_map/reduce_scatter | solution.py:81
  8.1 6.8 %collective-permute-start = (f32[1,12,1,128]{3,2,1,0:T(1,128)S(1)}, f32[1,12,1,128]{3,2,1,0:T(1,128)S(1)}, u32[]{:S(2)}, u32[]{:S(2)}) collective-permute-start(f32[1,12,1,128]{3,2,1,0:T(1,128)S(1)} %get-tuple-element.128), channel_id=1, source_target_pairs={{0,1},{2,3},{4,5},{6,7},{8,9},{10,11},{12,13},{14,15},{16,17},{18,... | collective-permute-start | bytes 18440 | tf_op jit(solution)/shard_map/ppermute | solution.py:19
  12.9 5.5 %collective-permute-start.1 = (f32[1,12,1,128]{3,2,1,0:T(1,128)S(1)}, f32[1,12,1,128]{3,2,1,0:T(1,128)S(1)}, u32[]{:S(2)}, u32[]{:S(2)}) collective-permute-start(f32[1,12,1,128]{3,2,1,0:T(1,128)S(1)} %get-tuple-element.129), channel_id=1, source_target_pairs={{1,0},{3,2},{5,4},{7,6},{9,8},{11,10},{13,12},{15,14},{17,16},{19,... | collective-permute-start | bytes 18440 | tf_op jit(solution)/shard_map/ppermute | solution.py:20
  21.3 69.5 %copy-start.2 = (f32[12,1,1152]{2,1,0:T(1,128)S(1)}, f32[12,1,1152]{2,1,0:T(1,128)}, u32[]{:S(2)}) copy-start(f32[12,1,1152]{2,1,0:T(1,128)} %param.28) | copy-start | bytes 165892
  80.5 4.3 %collective-permute-start.2 = (f32[12,1,8]{1,0,2:T(8,128)S(1)}, f32[12,1,8]{1,0,2:T(8,128)S(1)}, u32[]{:S(2)}, u32[]{:S(2)}) collective-permute-start(f32[12,1,8]{1,0,2:T(8,128)S(1)} %get-tuple-element.132), channel_id=1, source_target_pairs={{0,1},{1,0},{2,3},{3,2},{4,5},{5,4},{6,7},{7,6},{8,9},{9,8},{10,11... | collective-permute-start | bytes 1160 | tf_op jit(solution)/shard_map/ppermute | solution.py:19
  81.9 4.3 %collective-permute-start.3 = (f32[12,1,8]{1,0,2:T(8,128)S(1)}, f32[12,1,8]{1,0,2:T(8,128)S(1)}, u32[]{:S(2)}, u32[]{:S(2)}) collective-permute-start(f32[12,1,8]{1,0,2:T(8,128)S(1)} %get-tuple-element.133), channel_id=1, source_target_pairs={{1,0},{0,1},{3,2},{2,3},{5,4},{4,5},{7,6},{6,7},{9,8},{8,9},{11,10... | collective-permute-start | bytes 1160 | tf_op jit(solution)/shard_map/ppermute | solution.py:20
  86.3 5.8 %collective-permute-start.4 = (f32[12,18,1]{1,2,0:T(1,128)S(1)}, f32[12,18,1]{1,2,0:T(1,128)S(1)}, u32[]{:S(2)}, u32[]{:S(2)}) collective-permute-start(f32[12,18,1]{1,2,0:T(1,128)S(1)} %get-tuple-element.116), channel_id=1, source_target_pairs={{0,2},{2,4},{4,6},{6,8},{8,10},{10,12},{12,14},{14,16},{16,18},{18... | collective-permute-start | bytes 2600 | tf_op jit(solution)/shard_map/ppermute | solution.py:19
  86.4 5.8 %collective-permute-start.5 = (f32[12,18,1]{1,2,0:T(1,128)S(1)}, f32[12,18,1]{1,2,0:T(1,128)S(1)}, u32[]{:S(2)}, u32[]{:S(2)}) collective-permute-start(f32[12,18,1]{1,2,0:T(1,128)S(1)} %get-tuple-element.117), channel_id=1, source_target_pairs={{2,0},{4,2},{6,4},{8,6},{10,8},{12,10},{14,12},{16,14},{18,16},{20... | collective-permute-start | bytes 2600 | tf_op jit(solution)/shard_map/ppermute | solution.py:20
  91.2 12.2 %copy-start.5 = (f32[12,1,256]{2,1,0:T(1,128)S(1)}, f32[12,1,256]{2,1,0:T(1,128)}, u32[]{:S(2)}) copy-start(f32[12,1,256]{2,1,0:T(1,128)} %param.30) | copy-start | bytes 36868
  91.2 12.2 %copy-start.6 = (f32[1,256]{1,0:T(1,128)S(1)}, f32[1,256]{1,0:T(1,128)}, u32[]{:S(2)}) copy-start(f32[1,256]{1,0:T(1,128)} %param.31) | copy-start | bytes 3076
  91.2 12.2 %copy-start.7 = (s32[1,256]{1,0:T(1,128)S(1)}, s32[1,256]{1,0:T(1,128)}, u32[]{:S(2)}) copy-start(s32[1,256]{1,0:T(1,128)} %param.29) | copy-start | bytes 3076
  92.8 5.8 %collective-permute-start.6 = (f32[12,48,1]{1,2,0:T(1,128)S(1)}, f32[12,48,1]{1,2,0:T(1,128)S(1)}, u32[]{:S(2)}, u32[]{:S(2)}) collective-permute-start(f32[12,48,1]{1,2,0:T(1,128)S(1)} %get-tuple-element.114), channel_id=1, source_target_pairs={{2,0},{4,2},{6,4},{8,6},{10,8},{12,10},{14,12},{16,14},{18,16},{20... | collective-permute-start | bytes 6920 | tf_op jit(solution)/shard_map/ppermute | solution.py:20
  97.3 5.8 %collective-permute-start.7 = (f32[12,48,1]{1,2,0:T(1,128)S(1)}, f32[12,48,1]{1,2,0:T(1,128)S(1)}, u32[]{:S(2)}, u32[]{:S(2)}) collective-permute-start(f32[12,48,1]{1,2,0:T(1,128)S(1)} %get-tuple-element.115), channel_id=1, source_target_pairs={{0,2},{2,4},{4,6},{6,8},{8,10},{10,12},{12,14},{14,16},{16,18},{18... | collective-permute-start | bytes 6920 | tf_op jit(solution)/shard_map/ppermute | solution.py:19
  103.4 2.3 %copy-start.4 = (s32[3]{0:T(128)S(1)}, s32[3]{0:T(128)}, u32[]{:S(2)}) copy-start(s32[3]{0:T(128)} %constant.273.clone.1) | copy-start | bytes 40
  105.1 1.4 collective-permute-start.8
  105.2 5.8 %collective-permute-start.9 = (f32[12,48,1]{1,2,0:T(1,128)S(1)}, f32[12,48,1]{1,2,0:T(1,128)S(1)}, u32[]{:S(2)}, u32[]{:S(2)}) collective-permute-start(f32[12,48,1]{1,2,0:T(1,128)S(1)} %get-tuple-element.113), channel_id=1, source_target_pairs={{0,2},{2,4},{4,6},{6,8},{8,10},{10,12},{12,14},{14,16},{16,18},{18... | collective-permute-start | bytes 6920 | tf_op jit(solution)/shard_map/ppermute | solution.py:19
  111.6 4.5 %collective-permute-start.10 = (f32[12,1,10]{1,0,2:T(8,128)S(1)}, f32[12,1,10]{1,0,2:T(8,128)S(1)}, u32[]{:S(2)}, u32[]{:S(2)}) collective-permute-start(f32[12,1,10]{1,0,2:T(8,128)S(1)} %get-tuple-element.131), channel_id=1, source_target_pairs={{0,1},{1,0},{2,3},{3,2},{4,5},{5,4},{6,7},{7,6},{8,9},{9,8},{10,11... | collective-permute-start | bytes 1448 | tf_op jit(solution)/shard_map/ppermute | solution.py:19
  112.4 4.6 %collective-permute-start.11 = (f32[12,1,10]{1,0,2:T(8,128)S(1)}, f32[12,1,10]{1,0,2:T(8,128)S(1)}, u32[]{:S(2)}, u32[]{:S(2)}) collective-permute-start(f32[12,1,10]{1,0,2:T(8,128)S(1)} %get-tuple-element.130), channel_id=1, source_target_pairs={{1,0},{0,1},{3,2},{2,3},{5,4},{4,5},{7,6},{6,7},{9,8},{8,9},{11,10... | collective-permute-start | bytes 1448 | tf_op jit(solution)/shard_map/ppermute | solution.py:20
  117.1 5.8 %collective-permute-start.12 = (f32[12,20,1]{1,0,2:T(8,128)S(1)}, f32[12,20,1]{1,0,2:T(8,128)S(1)}, u32[]{:S(2)}, u32[]{:S(2)}) collective-permute-start(f32[12,20,1]{1,0,2:T(8,128)S(1)} %get-tuple-element.111), channel_id=1, source_target_pairs={{0,2},{2,4},{4,6},{6,8},{8,10},{10,12},{12,14},{14,16},{16,18},{18... | collective-permute-start | bytes 2888 | tf_op jit(solution)/shard_map/ppermute | solution.py:19
  117.1 5.8 %collective-permute-start.13 = (f32[12,20,1]{1,0,2:T(8,128)S(1)}, f32[12,20,1]{1,0,2:T(8,128)S(1)}, u32[]{:S(2)}, u32[]{:S(2)}) collective-permute-start(f32[12,20,1]{1,0,2:T(8,128)S(1)} %get-tuple-element.110), channel_id=1, source_target_pairs={{2,0},{4,2},{6,4},{8,6},{10,8},{12,10},{14,12},{16,14},{18,16},{20... | collective-permute-start | bytes 2888 | tf_op jit(solution)/shard_map/ppermute | solution.py:20
  147.2 5.2 %collective-permute-start.14 = (f32[1,12,1,128]{3,2,1,0:T(1,128)S(1)}, f32[1,12,1,128]{3,2,1,0:T(1,128)S(1)}, u32[]{:S(2)}, u32[]{:S(2)}) collective-permute-start(f32[1,12,1,128]{3,2,1,0:T(1,128)S(1)} %get-tuple-element.122), channel_id=1, source_target_pairs={{0,1},{2,3},{4,5},{6,7},{8,9},{10,11},{12,13},{14,15},{16,17},{18,... | collective-permute-start | bytes 18440 | tf_op jit(solution)/shard_map/ppermute | solution.py:19
  150.3 5.5 %collective-permute-start.15 = (f32[1,12,1,128]{3,2,1,0:T(1,128)S(1)}, f32[1,12,1,128]{3,2,1,0:T(1,128)S(1)}, u32[]{:S(2)}, u32[]{:S(2)}) collective-permute-start(f32[1,12,1,128]{3,2,1,0:T(1,128)S(1)} %get-tuple-element.123), channel_id=1, source_target_pairs={{1,0},{3,2},{5,4},{7,6},{9,8},{11,10},{13,12},{15,14},{17,16},{19,... | collective-permute-start | bytes 18440 | tf_op jit(solution)/shard_map/ppermute | solution.py:20
  (1 other events, 1.4 us)
Sparse Core Ops, SparseCore 0:
  21.4 57.9 reduce-scatter.1
where the time goes:
time: 164 us
  waiting for transfers between devices  81.9 us (50%)
  starting transfers between devices  28.7 us (18%)
  blocking collectives  20.1 us (12%)
  between operations  14.4 us (9%)
  local copies, waits for them, and re-layouts  9.68 us (6%)
  other arithmetic  6.44 us (4%)
  matrix products  2.43 us (1%)
    reduce_scatter x1, waiting for transfers between devices, shards(): lax.psum_scatter(partial_value, 'mem', scatter_dimension=2, tiled=True)  58.1 us
    all_gather x1, blocking collectives, shards(): coarse_gradient = lax.all_gather(own_block, 'mem', axis=2, tiled=True)  20.1 us
    ppermute x8, starting transfers between devices, padded_2(): after = lax.ppermute(initial, axis, down)  17.9 us
    ppermute x8, waiting for transfers between devices, padded_2(): before = lax.ppermute(last, axis, up)  13.2 us
    ppermute x8, starting transfers between devices, padded_2(): before = lax.ppermute(last, axis, up)  10.7 us
    ppermute x8, waiting for transfers between devices, padded_2(): after = lax.ppermute(initial, axis, down)  10.6 us
  transfers between devices with their start and end apart: 17, of which 13 were waited for; matrix products, arithmetic and copies ran while one was open for 3% of the time, Pallas kernels for 0%

commit v1 on v0

v1 whole, which is shorter than its diff:
```python
import functools
import math

import jax
import jax.numpy as jnp
from jax import lax
from jax.experimental import pallas as pl
from jax.experimental.pallas import tpu as pltpu
from jax.sharding import PartitionSpec as P

advect_rate = 0.25
LANES = 128
f32 = jnp.float32
bf16 = jnp.bfloat16


def split2(x):
    hi = x.astype(bf16)
    lo = (x - hi.astype(f32)).astype(bf16)
    return hi, lo


def dims(a, b, ca, cb):
    return lax.dot_general(a, b, (((ca,), (cb,)), ((), ())), preferred_element_type=f32)


def smooth_lon(x):
    n = x.shape[1]
    return 0.25 * pltpu.roll(x, 1, 1) + 0.5 * x + 0.25 * pltpu.roll(x, n - 1, 1)


def kernel(
    cfg,
    ens_ref,
    alpha_ref,
    low_ref,
    wt_ref,
    bg_ref,
    cell_ref,
    val_ref,
    prec_ref,
    adv_ref,
    grad_ref,
    ensf,
    edge_send,
    edge_recv,
    partial_rows,
    send1,
    recv1,
    sum1,
    place,
    table_hi,
    table_lo,
    frame_rows,
    frame_recv,
    send2,
    recv2,
    merged,
    coarse,
    edge_ss,
    edge_rs,
    frame_ss,
    frame_rs,
    ss1,
    rs1,
    ss2,
    rs2,
    bg_recv,
    bg_ss,
    bg_rs,
):
    n, nb, lev, rows, lon, fine_rows, fine_cols, scale = cfg
    block = lon // n
    frame = block + 2
    ratio = fine_cols // block
    cells = fine_rows * fine_cols
    wrows = recv1.shape[1]
    per = LANES // frame
    order = list(range(1, rows - 1)) + [-1, 0, rows - 1, rows]
    slot = {k: i for i, k in enumerate(order)}
    up_at = (rows - 2) * lev
    down_at = rows * lev
    groups = partial_rows.shape[0] // LANES
    me = lax.axis_index("mem")
    band = lax.axis_index("band")
    has_up = band > 0
    has_down = band < nb - 1

    barrier = pltpu.get_barrier_semaphore()

    def greet(o, c):
        pl.semaphore_signal(barrier, inc=1, device_id={"mem": lax.rem(me + o, n)})
        return c

    lax.fori_loop(1, n, greet, 0)

    @pl.when(has_up)
    def _():
        pl.semaphore_signal(barrier, inc=1, device_id={"band": band - 1})

    @pl.when(has_down)
    def _():
        pl.semaphore_signal(barrier, inc=1, device_id={"band": band + 1})

    ensf[...] = ens_ref[...].astype(f32)

    def row(ref, k):
        parts = [ref.at[t][pl.ds(k, lev, stride=rows), :] for t in range(lon // LANES)]
        return parts[0] if len(parts) == 1 else jnp.concatenate(parts, axis=1)

    for side, ks in ((0, (0, 1)), (1, (rows - 1, rows - 2))):
        edge_send[side, 0, 0:lev, :] = row(alpha_ref, ks[0])
        edge_send[side, 1, 0:lev, :] = row(alpha_ref, ks[1])
        edge_send[side, 2, 0:lev, :] = row(ensf, ks[0])

    if nb == 2:
        pl.semaphore_wait(barrier, n)
    else:
        pl.semaphore_wait(barrier, n - 1 + has_up.astype(jnp.int32) + has_down.astype(jnp.int32))

    def edge_copy(side):
        return pltpu.make_async_remote_copy(
            src_ref=edge_send.at[side],
            dst_ref=edge_recv.at[1 - side],
            send_sem=edge_ss.at[side],
            recv_sem=edge_rs.at[1 - side],
            device_id={"band": band - 1 if side == 0 else band + 1},
        )

    def frame_copy(side):
        at = up_at if side == 0 else down_at
        return pltpu.make_async_remote_copy(
            src_ref=frame_rows.at[pl.ds(at, 2 * lev), :],
            dst_ref=frame_recv.at[1 - side],
            send_sem=frame_ss.at[side],
            recv_sem=frame_rs.at[1 - side],
            device_id={"band": band - 1 if side == 0 else band + 1},
        )

    def start_band(copy, recv):
        for side, has in ((0, has_up), (1, has_down)):

            @pl.when(has)
            def _():
                copy(side).start()

            @pl.when(jnp.logical_not(has))
            def _():
                recv[side] = jnp.zeros(recv.shape[1:], f32)

    def wait_band(copy):
        for side, has in ((0, has_up), (1, has_down)):

            @pl.when(has)
            def _():
                copy(side).wait_send()
                copy(1 - side).wait_recv()

    start_band(edge_copy, edge_recv)

    def bg_copy(side):
        return pltpu.make_async_remote_copy(
            src_ref=bg_ref,
            dst_ref=bg_recv.at[1 - side],
            send_sem=bg_ss.at[side],
            recv_sem=bg_rs.at[1 - side],
            device_id={"mem": lax.rem(me + (n - 1 if side == 0 else 1), n)},
        )

    bg_copy(0).start()
    bg_copy(1).start()

    fr = lax.broadcasted_iota(jnp.int32, (fine_rows, cells), 0)
    fc = lax.broadcasted_iota(jnp.int32, (fine_rows, cells), 1)
    pick = (fc // fine_cols == fr).astype(bf16)
    w_hi = wt_ref[...].astype(bf16)
    rest = wt_ref[...] - w_hi.astype(f32)
    w_mid = rest.astype(bf16)
    w_lo = (rest - w_mid.astype(f32)).astype(bf16)
    low_b = low_ref[...].astype(f32).astype(bf16)
    rowvec = jnp.concatenate([jnp.broadcast_to(v, (8, fine_rows)) for v in (w_hi.astype(f32), w_mid.astype(f32), w_lo.astype(f32), low_b.astype(f32))], axis=0)
    spread = dims(rowvec.astype(bf16), pick, 1, 0)
    wcell = spread[0:1] + spread[8:9] + spread[16:17]
    lcell = spread[24:25].astype(jnp.int32)
    cell = lax.broadcasted_iota(jnp.int32, (1, cells), 1)
    col = cell % fine_cols

    def lon_parts(shift):
        num = 2 * (col + shift) + 1 + ratio
        return num // (2 * ratio), (num % (2 * ratio)).astype(f32) / (2 * ratio)

    q0, f0 = lon_parts(0)
    qn, fn = lon_parts(1)
    qp, fp = lon_parts(-1)
    chunk = 32

    def table_step(i, c):
        kap = lax.broadcasted_iota(jnp.int32, (chunk, 1), 0) + i * chunk
        lane = kap % LANES
        k = (kap // LANES) * per + lane // frame
        w = lane % frame
        ok = lane < per * frame
        k = jnp.where(ok, k, -5)
        w = jnp.where(ok, w, -5)
        latv = jnp.where(k == lcell + 1, 1.0 - wcell, 0.0) + jnp.where(k == lcell + 2, wcell, 0.0)

        def lonv(q, f):
            return jnp.where(w == q, 1.0 - f, 0.0) + jnp.where(w == q + 1, f, 0.0)

        at = pl.ds(pl.multiple_of(i * chunk, chunk), chunk)
        hi, lo = split2(latv * lonv(q0, f0))
        table_hi[at, 0:cells] = hi
        table_lo[at, 0:cells] = lo
        hi, lo = split2(latv * (0.5 * (lonv(qn, fn) - lonv(qp, fp))))
        table_hi[at, cells : 2 * cells] = hi
        table_lo[at, cells : 2 * cells] = lo
        return c

    lax.fori_loop(0, table_hi.shape[0] // chunk, table_step, 0)

    nobs = cell_ref.shape[1]
    prec = prec_ref[...]
    lhs = jnp.concatenate([prec * val_ref[:, 0, :], prec, jnp.zeros((16 - lev - 1, nobs), f32)], axis=0)
    l_hi = lhs.astype(bf16).astype(f32)
    l_mid = (lhs - l_hi).astype(bf16).astype(f32)
    l_lo = lhs - l_hi - l_mid
    l3 = jnp.concatenate([l_hi, l_mid, l_lo], axis=0).astype(bf16)
    hot = (lax.broadcasted_iota(jnp.int32, (cells, nobs), 0) == cell_ref[...]).astype(f32).astype(bf16)
    obs = dims(l3, hot, 1, 1)
    obs = obs[0:16] + obs[16:32] + obs[32:48]
    obs_b = obs[0:lev]
    obs_a = obs[lev : lev + 1]
    partial_rows[...] = jnp.zeros(partial_rows.shape, f32)
    frame_rows[...] = jnp.zeros(frame_rows.shape, f32)
    send1[...] = jnp.zeros(send1.shape, f32)
    send2[...] = jnp.zeros(send2.shape, f32)
    back = bg_ref[:, 0, :]
    for side in (0, 1):
        bg_copy(side).wait()
    from_left, from_right = bg_recv[0, :, 0, :], bg_recv[1, :, 0, :]
    before = jnp.where(col == 0, pltpu.roll(from_left, cells - fine_cols + 1, 1), pltpu.roll(back, 1, 1))
    after = jnp.where(
        col == fine_cols - 1, pltpu.roll(from_right, fine_cols - 1, 1), pltpu.roll(back, cells - 1, 1)
    )
    back_slope = 0.5 * (after - before)

    wait_band(edge_copy)

    def alpha_row(k):
        if k < 0:
            return edge_recv[0, -1 - k, 0:lev, :]
        if k >= rows:
            return edge_recv[1, k - rows, 0:lev, :]
        return row(alpha_ref, k)

    def ens_row(k):
        if k < 0:
            return edge_recv[0, 2, 0:lev, :]
        if k >= rows:
            return edge_recv[1, 2, 0:lev, :]
        return row(ensf, k)

    for k in range(-1, rows + 1):
        s = 0.25 * alpha_row(k - 1) + 0.5 * alpha_row(k) + 0.25 * alpha_row(k + 1)
        partial_rows[slot[k] * lev : (slot[k] + 1) * lev, :] = smooth_lon(s) * ens_row(k) * scale

    for g in range(groups):
        for t in range(lon // LANES):
            piece = partial_rows[g * LANES : (g + 1) * LANES, t * LANES : (t + 1) * LANES].T
            send1[pl.ds(groups * (t * LANES + 1) + g, LANES, stride=groups), :] = piece
    send1[0:groups, :] = send1[groups * lon : groups * (lon + 1), :]
    send1[groups * (lon + 1) : groups * (lon + 2), :] = send1[groups : 2 * groups, :]

    step = groups * block

    def copy1(dst):
        return pltpu.make_async_remote_copy(
            src_ref=send1.at[pl.ds(pl.multiple_of(dst * step, step), wrows), :],
            dst_ref=recv1.at[me],
            send_sem=ss1.at[dst],
            recv_sem=rs1.at[me],
            device_id={"mem": dst},
        )

    def copy2(dst):
        return pltpu.make_async_remote_copy(
            src_ref=send2,
            dst_ref=recv2.at[me],
            send_sem=ss2.at[dst],
            recv_sem=rs2.at[me],
            device_id={"mem": dst},
        )

    def start_all(copy):
        def go(o, c):
            copy(lax.rem(me + o, n)).start()
            return c

        lax.fori_loop(1, n, go, 0)

    def wait_all(copy, recv, ss, rs):
        def go(o, c):
            src = lax.rem(me + o, n)
            pltpu.make_async_copy(recv.at[src], recv.at[src], rs.at[src]).wait()
            copy(src).wait_send()
            return c

        lax.fori_loop(1, n, go, 0)

    start_all(copy1)
    recv1[me] = send1[pl.ds(pl.multiple_of(me * step, step), wrows), :]
    wait_all(copy1, recv1, ss1, rs1)
    total = recv1[0]
    for s in range(1, n):
        total = total + recv1[s]
    sum1[...] = total
    fr_pad = wrows // groups
    for g in range(groups):
        win = sum1[pl.ds(g, fr_pad, stride=groups), :]
        win = jnp.concatenate([win, jnp.zeros((LANES - fr_pad, LANES), f32)], axis=0)
        place[g * LANES : (g + 1) * LANES, :] = win.T

    lane16 = lax.broadcasted_iota(jnp.int32, (lev, LANES), 1)
    tiles = table_hi.shape[0] // LANES
    x_tiles = []
    for t in range(tiles):
        acc = jnp.zeros((lev, LANES), f32)
        for j in range(per):
            k = t * per + j - 1
            if k > rows:
                break
            piece = place[slot[k] * lev : (slot[k] + 1) * lev, :]
            if j:
                piece = pltpu.roll(piece, j * frame, 1)
            acc = jnp.where((lane16 >= j * frame) & (lane16 < (j + 1) * frame), piece, acc)
        x_tiles.append(acc)
    x = jnp.concatenate(x_tiles, axis=1)
    x = jnp.concatenate([x, jnp.zeros((16 - lev, x.shape[1]), f32)], axis=0)
    x_hi = x.astype(bf16).astype(f32)
    x2 = jnp.concatenate([x_hi, x - x_hi], axis=0).astype(bf16)
    y = dims(x2, table_hi[...], 1, 0)
    y = y[0:16] + y[16:32] + dims(x_hi.astype(bf16), table_lo[...], 1, 0)

    state = back + y[0:lev, 0:cells]
    slope = y[0:lev, cells : 2 * cells] + back_slope
    factor = 1.0 - advect_rate * slope
    moved = state * factor
    adv_ref[:, 0, :] = moved
    cot = obs_a * moved - obs_b
    uv = jnp.concatenate([cot * factor, (-advect_rate) * (state * cot)], axis=1)
    uv = jnp.concatenate([uv, jnp.zeros((16 - lev, 2 * cells), f32)], axis=0)
    uv_hi = uv.astype(bf16).astype(f32)
    uv2 = jnp.concatenate([uv_hi, uv - uv_hi], axis=0).astype(bf16)
    gr = dims(uv2, table_hi[...], 1, 1)
    gr = gr[0:16] + gr[16:32] + dims(uv_hi.astype(bf16), table_lo[...], 1, 1)
    for t in range(tiles):
        tile = gr[0:lev, t * LANES : (t + 1) * LANES]
        for j in range(per):
            k = t * per + j - 1
            if k > rows:
                break
            piece = tile if j == 0 else pltpu.roll(tile, LANES - j * frame, 1)
            piece = jnp.where(lane16 < frame, piece, 0.0)
            frame_rows[slot[k] * lev : (slot[k] + 1) * lev, :] = piece

    start_band(frame_copy, frame_recv)
    wait_band(frame_copy)
    frame_rows[up_at : up_at + 2 * lev, :] += frame_recv[0]
    frame_rows[down_at : down_at + 2 * lev, :] += frame_recv[1]
    for g in range(groups):
        send2[pl.ds(g, fr_pad, stride=groups), :] = frame_rows[g * LANES : (g + 1) * LANES, :].T[0:fr_pad]
    start_all(copy2)
    recv2[me] = send2[...]
    wait_all(copy2, recv2, ss2, rs2)

    over = wrows - step
    for d in range(n):
        merged[d * step : (d + 1) * step, :] = recv2[d, 0:step, :]
    for d in range(n):
        e = (d + 1) % n
        merged[e * step : e * step + over, :] += recv2[d, step:wrows, :]
    for g in range(groups):
        for t in range(lon // LANES):
            piece = merged[pl.ds(groups * t * LANES + g, LANES, stride=groups), :].T
            coarse[g * LANES : (g + 1) * LANES, t * LANES : (t + 1) * LANES] = piece

    def weighted(k):
        cg = coarse[slot[k] * lev : (slot[k] + 1) * lev, :]
        return ens_row(k) * pltpu.roll(cg, lon - 1, 1) * scale

    a, b = weighted(-1), weighted(0)
    for k in range(rows):
        c = weighted(k + 1)
        z = smooth_lon(0.25 * a + 0.5 * b + 0.25 * c)
        for t in range(lon // LANES):
            grad_ref.at[t][pl.ds(k, lev, stride=rows), :] = z[:, t * LANES : (t + 1) * LANES]
        a, b = b, c


def up_to(x, m):
    return -(-x // m) * m


def to_tiles(x):
    return x.reshape(-1, x.shape[3] // LANES, LANES).swapaxes(0, 1)


def shards(ensemble, alpha, lat_lower, lat_weight, background, obs_cell, obs_value, obs_precision):
    n, nb = lax.axis_size("mem"), lax.axis_size("band")
    members, lev, rows, lon = ensemble.shape
    fine_rows = lat_lower.shape[0]
    cells = background.shape[2]
    scale = 1.0 / math.sqrt(members * n - 1)
    block = lon // n
    frame = block + 2
    groups = up_to((rows + 2) * lev, LANES) // LANES
    wrows = up_to(groups * frame, 8 * groups // math.gcd(8, groups))
    per = LANES // frame
    kaps = -(-(rows + 2) // per) * LANES
    cfg = (n, nb, lev, rows, lon, fine_rows, cells // fine_rows, scale)
    levp = up_to(lev, 8)
    dma = pltpu.SemaphoreType.DMA
    vm = pl.BlockSpec(memory_space=pltpu.VMEM)
    advected, gradient = pl.pallas_call(
        functools.partial(kernel, cfg),
        out_shape=(
            jax.ShapeDtypeStruct(background.shape, f32),
            jax.ShapeDtypeStruct((lon // LANES, lev * rows, LANES), f32),
        ),
        in_specs=[vm] * 8,
        out_specs=(vm, vm),
        scratch_shapes=[
            pltpu.VMEM((lon // LANES, lev * rows, LANES), f32),
            pltpu.VMEM((2, 3, levp, lon), f32),
            pltpu.VMEM((2, 3, levp, lon), f32),
            pltpu.VMEM((groups * LANES, lon), f32),
            pltpu.VMEM((groups * lon + wrows, LANES), f32),
            pltpu.VMEM((n, wrows, LANES), f32),
            pltpu.VMEM((wrows, LANES), f32),
            pltpu.VMEM((groups * LANES, LANES), f32),
            pltpu.VMEM((kaps, 2 * cells), bf16),
            pltpu.VMEM((kaps, 2 * cells), bf16),
            pltpu.VMEM((groups * LANES, LANES), f32),
            pltpu.VMEM((2, 2 * lev, LANES), f32),
            pltpu.VMEM((wrows, LANES), f32),
            pltpu.VMEM((n, wrows, LANES), f32),
            pltpu.VMEM((groups * lon, LANES), f32),
            pltpu.VMEM((groups * LANES, lon), f32),
            dma((2,)),
            dma((2,)),
            dma((2,)),
            dma((2,)),
            dma((n,)),
            dma((n,)),
            dma((n,)),
            dma((n,)),
            pltpu.VMEM((2,) + background.shape, f32),
            dma((2,)),
            dma((2,)),
        ],
        compiler_params=pltpu.CompilerParams(collective_id=0, has_side_effects=True, vmem_limit_bytes=48 * 2**20),
    )(
        to_tiles(ensemble),
        to_tiles(alpha),
        lat_lower.reshape(1, fine_rows),
        lat_weight.reshape(1, fine_rows),
        background,
        obs_cell,
        obs_value,
        obs_precision,
    )
    return advected, gradient.swapaxes(0, 1).reshape(members, lev, rows, lon)


def solution(mesh):
    return jax.shard_map(
        shards,
        mesh=mesh,
        in_specs=(
            P("mem", None, "band", None),
            P("mem", None, "band", None),
            P("band"),
            P("band"),
            P(None, ("band", "mem"), None),
            P(("band", "mem"), None),
            P(None, ("band", "mem"), None),
            P(("band", "mem"), None),
        ),
        out_specs=(P(None, ("band", "mem"), None), P("mem", None, "band", None)),
        check_vma=False,
    )
```

time: 164 us -> 32.2 us (0.20)
  waiting for transfers between devices: 81.9 us -> 0 us
  starting transfers between devices: 28.7 us -> 0 us
  Pallas kernels: 0 us -> 26.1 us
  blocking collectives: 20.1 us -> 0 us
  between operations: 14.4 us -> 0.68 us
  other arithmetic: 6.44 us -> 0 us
  local copies, waits for them, and re-layouts: 9.68 us -> 5.16 us
  matrix products: 2.43 us -> 0 us
    reduce_scatter x1 -> x0, waiting for transfers between devices: 58.1 us -> none  [shards(): lax.psum_scatter(partial_value, 'mem', scatter_dimension=2, tiled=True)]
    ppermute x16 -> x0, starting transfers between devices: 28.6 us -> none  [the longest x8 17.9 us: padded_2(): after = lax.ppermute(initial, axis, down)]
    pallas_call x0 -> x1, Pallas kernels: none -> 26.1 us  [shards(): pl.pallas_call(functools.partial(kernel, cfg), out_shape=(jax.ShapeDtypeS...]
    ppermute x16 -> x0, waiting for transfers between devices: 23.7 us -> none  [the longest x8 13.2 us: padded_2(): before = lax.ppermute(last, axis, up)]
    all_gather x1 -> x0, blocking collectives: 20.1 us -> none  [shards(): coarse_gradient = lax.all_gather(own_block, 'mem', axis=2, tiled=True)]
    unnamed x16 -> x18, local copies, waits for them, and re-layouts: 0.05 us -> 5.16 us
    add x9 -> x0, other arithmetic: 2.88 us -> none  [the longest x2 1.14 us: smooth_local(): 0.25 * padded[:, :, :-2] + 0.5 * padded[:, :, 1:-1]]
    another operation x3 -> x0, other arithmetic: 2.78 us -> none
  transfers between devices with their start and end apart: 17 -> 0, of which waited for: 13 -> 0; matrix products, arithmetic and copies ran while one was open for 3% -> 0% of each run, Pallas kernels for 0% -> 0%
where the time goes in v1:
time: 32.2 us; the launch traced here: 31.9 us
  Pallas kernels  26.1 us (81%)
  local copies, waits for them, and re-layouts  5.16 us (16%)
  between operations  0.68 us (2%)
    pallas_call x1, Pallas kernels, shards(): pl.pallas_call(functools.partial(kernel, cfg), out_shape=(jax.ShapeDtypeS...  26.1 us
    unnamed x18, local copies, waits for them, and re-layouts  5.16 us

profile of v1, /device:TPU:0, one launch (start us, length us, event | category | flops | bytes accessed | tf_op | source)
XLA Modules:
  0.0 31.9 jit_solution(16420013504503717961)
XLA Ops:
  0.6 0.0 copy-start.5
  0.6 0.0 copy-start.7
  0.7 0.0 copy-start.4
  0.7 0.0 copy-start.6
  0.7 0.6 %copy-done.5 = f32[1,256]{1,0:T(1,128)S(1)} copy-done((f32[1,256]{1,0:T(1,128)S(1)}, f32[1,256]{1,0:T(1,128)}, u32[]{:S(2)}) %copy-start.5) | copy-done | bytes 1048
  1.3 0.0 copy-done.7
  1.3 0.0 copy-done.4
  1.3 0.0 copy-done.6
  1.3 0.0 copy-start
  1.3 0.9 %copy-done = f32[1,12,16,128]{3,2,1,0:T(8,128)S(1)} copy-done((f32[1,12,16,128]{3,2,1,0:T(8,128)S(1)}, f32[1,12,16,128]{3,2,1,0:T(8,128)}, u32[]{:S(2)}) %copy-start) | copy-done | bytes 98328
  2.2 0.0 copy-start.1
  2.2 0.8 %copy-done.1 = f32[12,1,1152]{2,1,0:T(1,128)S(1)} copy-done((f32[12,1,1152]{2,1,0:T(1,128)S(1)}, f32[12,1,1152]{2,1,0:T(1,128)}, u32[]{:S(2)}) %copy-start.1) | copy-done | bytes 55320
  3.1 0.0 copy-start.2
  3.1 0.8 %copy-done.2 = bf16[1,12,16,128]{3,2,1,0:T(8,128)(2,1)S(1)} copy-done((bf16[1,12,16,128]{3,2,1,0:T(8,128)(2,1)S(1)}, bf16[1,12,16,128]{3,2,1,0:T(8,128)(2,1)}, u32[]{:S(2)}) %copy-start.2) | copy-done | bytes 49176
  3.9 0.0 copy-start.3
  3.9 0.7 %copy-done.3 = f32[12,1,256]{2,1,0:T(1,128)S(1)} copy-done((f32[12,1,256]{2,1,0:T(1,128)S(1)}, f32[12,1,256]{2,1,0:T(1,128)}, u32[]{:S(2)}) %copy-start.3) | copy-done | bytes 12312
  4.6 26.1 %shard_map.95 = (f32[12,1,1152]{2,1,0:T(1,128)S(1)}, f32[1,192,128]{2,1,0:T(8,128)S(1)}) custom-call(bf16[1,192,128]{2,1,0:T(8,128)(2,1)S(1)} %bitcast.7, f32[1,192,128]{2,1,0:T(8,128)S(1)} %bitcast.5, s32[1,48]{1,0:T(1,128)S(1)} %bitcast.8, f32[1,48]{1,0:T(1,128)S(1)} %bitcast.9, f32[12,1,1152]{2,1,0:T(1,128)S(1)} %copy-done.1, s32[1,256]{1,0:T(1,128)S(1)} %copy-done.4, ...), custom_call_target="tpu_custom_call" | custom-call | tf_op jit(solution)/shard_map/pallas_call | solution.py:424
  30.6 0.6 %copy.12 = f32[12,1,1152]{2,1,0:T(1,128)} copy(f32[12,1,1152]{2,1,0:T(1,128)S(1)} %get-tuple-element.8) | data formatting | bytes 110592
  31.2 0.6 %copy.13 = f32[1,12,16,128]{3,2,1,0:T(8,128)} copy(f32[1,12,16,128]{3,2,1,0:T(8,128)S(1)} %bitcast.6) | data formatting | bytes 196608
Async XLA Ops:
  0.6 0.7 %copy-start.5 = (f32[1,256]{1,0:T(1,128)S(1)}, f32[1,256]{1,0:T(1,128)}, u32[]{:S(2)}) copy-start(f32[1,256]{1,0:T(1,128)} %prec_ref.1) | copy-start | bytes 3076
  0.6 0.7 %copy-start.7 = (f32[48]{0:T(128)S(1)}, f32[48]{0:T(128)}, u32[]{:S(2)}) copy-start(f32[48]{0:T(128)} %param.11) | copy-start | bytes 580
  0.7 0.7 %copy-start.4 = (s32[1,256]{1,0:T(1,128)S(1)}, s32[1,256]{1,0:T(1,128)}, u32[]{:S(2)}) copy-start(s32[1,256]{1,0:T(1,128)} %cell_ref.1) | copy-start | bytes 3076
  0.7 0.7 %copy-start.6 = (s32[48]{0:T(128)S(1)}, s32[48]{0:T(128)}, u32[]{:S(2)}) copy-start(s32[48]{0:T(128)} %param.10) | copy-start | bytes 580
  1.3 0.9 %copy-start = (f32[1,12,16,128]{3,2,1,0:T(8,128)S(1)}, f32[1,12,16,128]{3,2,1,0:T(8,128)}, u32[]{:S(2)}) copy-start(f32[1,12,16,128]{3,2,1,0:T(8,128)} %param.9) | copy-start | bytes 294916
  2.2 0.8 %copy-start.1 = (f32[12,1,1152]{2,1,0:T(1,128)S(1)}, f32[12,1,1152]{2,1,0:T(1,128)}, u32[]{:S(2)}) copy-start(f32[12,1,1152]{2,1,0:T(1,128)} %bg_ref.1) | copy-start | bytes 165892
  3.1 0.8 %copy-start.2 = (bf16[1,12,16,128]{3,2,1,0:T(8,128)(2,1)S(1)}, bf16[1,12,16,128]{3,2,1,0:T(8,128)(2,1)}, u32[]{:S(2)}) copy-start(bf16[1,12,16,128]{3,2,1,0:T(8,128)(2,1)} %param.8) | copy-start | bytes 147460
  3.9 0.7 %copy-start.3 = (f32[12,1,256]{2,1,0:T(1,128)S(1)}, f32[12,1,256]{2,1,0:T(1,128)}, u32[]{:S(2)}) copy-start(f32[12,1,256]{2,1,0:T(1,128)} %val_ref.1) | copy-start | bytes 36868
